TPU v7x, 32 devices: a whole 2x2x4 slice. The times are simulated.
32 devices in a mesh: dp: 16 (over z, y, core), tensor: 2 (over x).
Axes of the slice: x: 2, y: 2, z: 4, core: 2. Of those that a mesh axis runs over, the one named last changes fastest.
Arguments:
- step: int32 [1], replicated, may hold values from 0 to 999
- activations: bfloat16 [2, 16384, 8192], P(None, 'dp', 'tensor'), may hold values from -6 to 6
- grad_weight: bfloat16 [2, 8192, 28672], P(None, 'tensor', 'dp'), may hold values from -6 to 6
Outputs:
- preconditioned: float32 [8192, 28672], P('tensor', 'dp')
All inputs are finite; a program needn't handle non-finite values.
Results may differ from a plain program's by a relative error of at most 0.0044.
Values may be sent and summed in bfloat16 or wider, within the bound.
No kernel may reach another device: no remote copies, remote signals or barrier semaphores. Data moves between devices by JAX's collectives and lax.ppermute only.
A program may use at most 192 MiB of HBM per device.

v0:
```python
import jax
import jax.numpy as jnp
from jax import lax
from jax.sharding import PartitionSpec as P

BLOCK = 1024
LAYERS = 2
ITERS = 4


def local(step, activations, grad_weight):
    groups = lax.axis_size("dp")
    layer = step[0] % LAYERS
    damping = 0.05 + 0.1 * step[0].astype(jnp.float32) / 1000.0
    acts = lax.dynamic_index_in_dim(activations, layer, 0, keepdims=False)
    grads = lax.dynamic_index_in_dim(grad_weight, layer, 0, keepdims=False)
    tok_rows = acts.shape[0]
    width = acts.shape[1]
    nblock = width // BLOCK
    share = BLOCK // groups
    blocks = acts.reshape(tok_rows, nblock, BLOCK)
    total_tokens = tok_rows * groups
    first = lax.axis_index("dp") * share
    summed = lax.psum(
        jnp.einsum("tkr,tkc->rkc", blocks, blocks, preferred_element_type=jnp.float32), "dp"
    )
    gram_rows = lax.dynamic_slice_in_dim(summed, first, share, 0)
    row_ids = first + lax.broadcasted_iota(jnp.int32, (share, 1, BLOCK), 0)
    col_ids = lax.broadcasted_iota(jnp.int32, (share, 1, BLOCK), 2)
    identity = (row_ids == col_ids).astype(jnp.float32)
    factor = gram_rows / total_tokens + damping * identity
    block_squares = lax.psum(jnp.sum(factor * factor, axis=(0, 2)), "dp")
    largest = lax.pmax(jnp.max(block_squares), "tensor")
    iterate = jnp.broadcast_to(identity / jnp.sqrt(largest), factor.shape)
    for sweep in range(ITERS):
        whole = lax.all_gather(iterate, "dp", axis=0, tiled=True)
        product = jnp.einsum("rkj,jkc->rkc", factor, whole, precision=lax.Precision.HIGHEST)
        iterate = 2.0 * iterate - jnp.einsum(
            "rkj,jkc->rkc", product, whole, precision=lax.Precision.HIGHEST
        )
    inverse = iterate.astype(jnp.bfloat16)
    stacked = grads.reshape(nblock, BLOCK, grads.shape[1])
    result = jnp.einsum(
        "rkc,kcf->krf",
        lax.all_gather(inverse, "dp", axis=0, tiled=True),
        stacked,
        preferred_element_type=jnp.float32,
    )
    return result.reshape(width, grads.shape[1])


def solution(mesh):
    in_specs = (P(), P(None, "dp", "tensor"), P(None, "tensor", "dp"))
    out_specs = P("tensor", "dp")
    return jax.shard_map(local, mesh=mesh, in_specs=in_specs, out_specs=out_specs, check_vma=False)
```

profile of v0, /device:TPU:0, one launch (start us, length us, event | category | flops | bytes accessed | tf_op | source)
XLA Modules:
  0.0 1019.5 jit_solution(3891566731821359104)
XLA Ops:
  6.5 0.0 all-reduce.2.cloned.1.call-start
  7.2 7.9 constant_dynamic-slice_fusion.1
  15.1 12.0 %copy.23 = bf16[1,1024,4096]{1,2,0:T(8,128)(2,1)} copy(bf16[1,1024,4096]{2,1,0:T(8,128)(2,1)} %constant_dynamic-slice_fusion.1) | data formatting | bytes 16777216
  27.1 17.1 %convolution_bitcast_fusion = f32[1024,4,1024]{2,0,1:T(8,128)} fusion(bf16[1024,4,1024]{0,2,1:T(8,128)(2,1)} %bitcast.51), kind=kOutput, calls=%fused_computation | convolution fusion | flops 8589934592 | bytes 25165824 | tf_op jit(solution)/shard_map/tkr,tkc->rkc/dot_general | solution.py:25
  44.2 0.0 all-reduce.2.cloned.1.call-update
  44.3 0.0 all-gather.14.cloned.1.call-start
  44.3 0.1 fusion.18
  44.4 300.7 %all-reduce.2.cloned.1.call-done = f32[1024,4,1024]{2,0,1:T(8,128)} async-done(((f32[1024,4,1024]{2,0,1:T(8,128)}), f32[1024,4,1024]{2,0,1:T(8,128)}) %all-reduce.2.cloned.1.call-update) | async-done | bytes 16777232 | tf_op jit(solution)/shard_map/psum | solution.py:24
  345.1 1.5 multiply_reduce_fusion
  346.6 31.8 %psum.15 = f32[4]{0:T(128)S(1)} all-reduce(f32[4]{0:T(128)S(1)} %multiply_reduce_fusion), channel_id=1, replica_groups=mesh['dp'=16,'tensor'=2] {'dp'}, use_global_device_ids=true, to_apply=%region_2.3 | all-reduce | flops 4 | bytes 32 | tf_op jit(solution)/shard_map/psum | solution.py:32
  378.4 0.6 reduce_max.9
  379.0 5.5 pmax.7
  385.2 0.8 broadcast_multiply_fusion
  386.0 0.0 all-gather.14.cloned.1.call-update
  386.0 0.3 all-gather.6.cloned.1.call-start
  386.3 47.5 %all-gather.14.cloned.1.call-done = f32[1024,1024]{1,0:T(8,128)} async-done(((f32[64,1024]{1,0:T(8,128)}), f32[1024,1024]{1,0:T(8,128)}) %all-gather.14.cloned.1.call-update) | async-done | bytes 4194320 | tf_op jit(solution)/shard_map/all_gather | solution.py:36
  433.8 11.8 %fusion.4 = f32[64,4,1024]{2,0,1:T(8,128)S(1)} fusion(f32[1024,1024]{1,0:T(8,128)} %all-gather.14.cloned.1.call-done, f32[1024,4,1024]{2,0,1:T(8,128)} %all-reduce.2.cloned.1.call-done, s32[]{:T(128)S(6)} %select_n.18, f32[64,1024]{1,0:T(8,128)S(1)} %fusion.18), kind=kOutput, calls=%fused_computation.5 | convolution fusion | flops 3221749760 | bytes 6553604 | tf_op jit(solution)/shard_map/rkj,jkc->rkc/dot_general | solution.py:37
  445.6 12.8 %fusion.10 = f32[64,4,1024]{2,0,1:T(8,128)} fusion(f32[64,4,1024]{2,0,1:T(8,128)S(1)} %fusion.4, f32[1024,1024]{1,0:T(8,128)} %all-gather.14.cloned.1.call-done, f32[64,1024]{1,0:T(8,128)S(1)} %get-tuple-element.5), kind=kOutput, calls=%fused_computation.7 | convolution fusion | flops 3221487616 | bytes 6553600 | tf_op jit(solution)/shard_map/rkj,jkc->rkc/dot_general | solution.py:38
  458.3 0.0 copy-start.4
  458.3 0.0 all-gather.6.cloned.1.call-update
  458.4 0.0 all-gather.8.cloned.1.call-start
  458.4 125.1 %all-gather.6.cloned.1.call-done = f32[1024,4,1024]{2,0,1:T(8,128)} async-done(((f32[64,4,1024]{2,0,1:T(8,128)}), f32[1024,4,1024]{2,0,1:T(8,128)}) %all-gather.6.cloned.1.call-update) | async-done | bytes 16777232 | tf_op jit(solution)/shard_map/all_gather | solution.py:36
  583.5 0.0 copy-start.1
  583.5 15.3 %convolution_bitcast_fusion.6 = f32[64,4,1024]{2,0,1:T(8,128)S(1)} fusion(f32[1024,4,1024]{2,0,1:T(8,128)} %all-gather.6.cloned.1.call-done, f32[1024,4,1024]{2,0,1:T(8,128)} %all-reduce.2.cloned.1.call-done, s32[]{:T(128)S(6)} %select_n.18, f32[64,1024]{1,0:T(8,128)S(1)} %fusion.18), kind=kOutput, calls=%fused_computation.16 | convolution fusion | flops 3221749760 | bytes 19136516 | tf_op jit(solution)/shard_map/rkj,jkc->rkc/dot_general | solution.py:37
  598.8 0.0 copy-done.4
  598.8 0.0 copy-done.1
  598.8 11.8 %fusion.15 = f32[64,4,1024]{2,0,1:T(8,128)} fusion(f32[1024,4,1024]{2,0,1:T(8,128)S(1)} %copy-done.1, f32[64,4,1024]{2,0,1:T(8,128)S(1)} %convolution_bitcast_fusion.6, f32[64,4,1024]{2,0,1:T(8,128)S(1)} %copy-done.4), kind=kOutput, calls=%fused_computation.15 | convolution fusion | flops 3221749760 | bytes 19922944 | tf_op jit(solution)/shard_map/rkj,jkc->rkc/dot_general | solution.py:38
  610.6 0.0 copy-start.5
  610.6 0.0 all-gather.8.cloned.1.call-update
  610.6 0.0 all-gather.10.cloned.1.call-start
  610.7 124.7 %all-gather.8.cloned.1.call-done = f32[1024,4,1024]{2,0,1:T(8,128)} async-done(((f32[64,4,1024]{2,0,1:T(8,128)}), f32[1024,4,1024]{2,0,1:T(8,128)}) %all-gather.8.cloned.1.call-update) | async-done | bytes 16777232 | tf_op jit(solution)/shard_map/all_gather | solution.py:36
  735.4 0.0 copy-start.2
  735.4 15.0 %convolution_bitcast_fusion.4 = f32[64,4,1024]{2,0,1:T(8,128)S(1)} fusion(f32[1024,4,1024]{2,0,1:T(8,128)} %all-gather.8.cloned.1.call-done, f32[1024,4,1024]{2,0,1:T(8,128)} %all-reduce.2.cloned.1.call-done, s32[]{:T(128)S(6)} %select_n.18, f32[64,1024]{1,0:T(8,128)S(1)} %fusion.18), kind=kOutput, calls=%fused_computation.13 | convolution fusion | flops 3221749760 | bytes 19136516 | tf_op jit(solution)/shard_map/rkj,jkc->rkc/dot_general | solution.py:37
  750.4 0.0 copy-done.5
  750.4 0.0 copy-done.2
  750.4 11.8 %fusion.14 = f32[64,4,1024]{2,0,1:T(8,128)} fusion(f32[1024,4,1024]{2,0,1:T(8,128)S(1)} %copy-done.2, f32[64,4,1024]{2,0,1:T(8,128)S(1)} %convolution_bitcast_fusion.4, f32[64,4,1024]{2,0,1:T(8,128)S(1)} %copy-done.5), kind=kOutput, calls=%fused_computation.12 | convolution fusion | flops 3221749760 | bytes 19922944 | tf_op jit(solution)/shard_map/rkj,jkc->rkc/dot_general | solution.py:38
  762.2 0.0 copy-start.3
  762.2 0.0 all-gather.10.cloned.1.call-update
  762.2 0.0 all-gather.12.cloned.1.call-start
  762.3 124.7 %all-gather.10.cloned.1.call-done = f32[1024,4,1024]{2,0,1:T(8,128)} async-done(((f32[64,4,1024]{2,0,1:T(8,128)}), f32[1024,4,1024]{2,0,1:T(8,128)}) %all-gather.10.cloned.1.call-update) | async-done | bytes 16777232 | tf_op jit(solution)/shard_map/all_gather | solution.py:36
  887.0 0.0 copy-start
  887.0 15.0 %convolution_bitcast_fusion.2 = f32[64,4,1024]{2,0,1:T(8,128)S(1)} fusion(f32[1024,4,1024]{2,0,1:T(8,128)} %all-gather.10.cloned.1.call-done, f32[1024,4,1024]{2,0,1:T(8,128)} %all-reduce.2.cloned.1.call-done, s32[]{:T(128)S(6)} %select_n.18, f32[64,1024]{1,0:T(8,128)S(1)} %fusion.18), kind=kOutput, calls=%fused_computation.10 | convolution fusion | flops 3221749760 | bytes 19136516 | tf_op jit(solution)/shard_map/rkj,jkc->rkc/dot_general | solution.py:37
  902.0 0.0 copy-done.3
  902.0 0.0 copy-done
  902.0 11.6 %fusion.16 = bf16[64,4,1024]{2,0,1:T(8,128)(2,1)} fusion(f32[1024,4,1024]{2,0,1:T(8,128)S(1)} %copy-done, f32[64,4,1024]{2,0,1:T(8,128)S(1)} %convolution_bitcast_fusion.2, f32[64,4,1024]{2,0,1:T(8,128)S(1)} %copy-done.3), kind=kOutput, calls=%fused_computation.17 | convolution fusion | flops 3222011904 | bytes 19398656 | tf_op jit(solution)/shard_map/rkj,jkc->rkc/dot_general | solution.py:38
  913.7 0.0 all-gather.12.cloned.1.call-update
  913.7 13.2 %constant_dynamic-slice_fusion = bf16[1,4096,1792]{2,1,0:T(8,128)(2,1)} fusion(bf16[2,4096,1792]{2,1,0:T(8,128)(2,1)} %param.5, s32[]{:T(128)S(6)} %select_n.17), kind=kLoop, calls=%fused_computation.24 | loop fusion | bytes 29360132 | tf_op jit(solution)/shard_map/jit(dynamic_index_in_dim)/dynamic_slice | solution.py:16
  926.9 59.4 %all-gather.12.cloned.1.call-done = bf16[1024,4,1024]{2,0,1:T(8,128)(2,1)} async-done(((bf16[64,4,1024]{2,0,1:T(8,128)(2,1)}), bf16[1024,4,1024]{2,0,1:T(8,128)(2,1)}) %all-gather.12.cloned.1.call-update) | async-done | bytes 8388624 | tf_op jit(solution)/shard_map/all_gather | solution.py:45
  986.3 25.9 %fusion.19 = f32[4,1024,1792]{2,1,0:T(8,128)} fusion(bf16[1024,4,1024]{2,0,1:T(8,128)(2,1)} %all-gather.12.cloned.1.call-done, bf16[4,1024,1792]{2,1,0:T(8,128)(2,1)} %bitcast.50), kind=kOutput, calls=%fused_computation.27 | convolution fusion | flops 15032385536 | bytes 52428800 | tf_op jit(solution)/shard_map/rkc,kcf->krf/dot_general | solution.py:43
  (1 shorter events, 0.0 us)
Async XLA Ops:
  6.5 338.6 %all-reduce.2.cloned.1.call-start = ((), (), s32[]{:S(2)}) async-start(), calls=%async_computation | async-start | bytes 33554432 | tf_op jit(solution)/shard_map/psum | solution.py:24
  44.3 389.5 %all-gather.14.cloned.1.call-start = ((), (), s32[]{:S(2)}) async-start(), calls=%async_computation.5 | async-start | bytes 4456448 | tf_op jit(solution)/shard_map/all_gather | solution.py:36
  386.0 197.5 %all-gather.6.cloned.1.call-start = ((), (), s32[]{:S(2)}) async-start(), calls=%async_computation.1 | async-start | bytes 17825792 | tf_op jit(solution)/shard_map/all_gather | solution.py:36
  458.3 140.4 %copy-start.4 = (f32[64,4,1024]{2,0,1:T(8,128)S(1)}, f32[64,4,1024]{2,0,1:T(8,128)}, u32[]{:S(2)}) copy-start(f32[64,4,1024]{2,0,1:T(8,128)} %fusion.10) | copy-start | bytes 3145732
  458.4 277.0 %all-gather.8.cloned.1.call-start = ((), (), s32[]{:S(2)}) async-start(), calls=%async_computation.2 | async-start | bytes 17825792 | tf_op jit(solution)/shard_map/all_gather | solution.py:36
  583.5 15.3 %copy-start.1 = (f32[1024,4,1024]{2,0,1:T(8,128)S(1)}, f32[1024,4,1024]{2,0,1:T(8,128)}, u32[]{:S(2)}) copy-start(f32[1024,4,1024]{2,0,1:T(8,128)} %all-gather.6.cloned.1.call-done) | copy-start | bytes 50331652
  610.6 139.8 %copy-start.5 = (f32[64,4,1024]{2,0,1:T(8,128)S(1)}, f32[64,4,1024]{2,0,1:T(8,128)}, u32[]{:S(2)}) copy-start(f32[64,4,1024]{2,0,1:T(8,128)} %fusion.15) | copy-start | bytes 3145732
  610.6 276.4 %all-gather.10.cloned.1.call-start = ((), (), s32[]{:S(2)}) async-start(), calls=%async_computation.3 | async-start | bytes 17825792 | tf_op jit(solution)/shard_map/all_gather | solution.py:36
  735.4 15.0 %copy-start.2 = (f32[1024,4,1024]{2,0,1:T(8,128)S(1)}, f32[1024,4,1024]{2,0,1:T(8,128)}, u32[]{:S(2)}) copy-start(f32[1024,4,1024]{2,0,1:T(8,128)} %all-gather.8.cloned.1.call-done) | copy-start | bytes 50331652
  762.2 139.8 %copy-start.3 = (f32[64,4,1024]{2,0,1:T(8,128)S(1)}, f32[64,4,1024]{2,0,1:T(8,128)}, u32[]{:S(2)}) copy-start(f32[64,4,1024]{2,0,1:T(8,128)} %fusion.14) | copy-start | bytes 3145732
  762.2 224.1 %all-gather.12.cloned.1.call-start = ((), (), s32[]{:S(2)}) async-start(), calls=%async_computation.4 | async-start | bytes 8912896 | tf_op jit(solution)/shard_map/all_gather | solution.py:45
  887.0 15.0 %copy-start = (f32[1024,4,1024]{2,0,1:T(8,128)S(1)}, f32[1024,4,1024]{2,0,1:T(8,128)}, u32[]{:S(2)}) copy-start(f32[1024,4,1024]{2,0,1:T(8,128)} %all-gather.10.cloned.1.call-done) | copy-start | bytes 50331652
Sparse Core Ops, SparseCore 0:
  44.4 300.6 all-reduce.1
  386.1 47.5 all-gather.13
  458.5 124.9 all-gather.5
  610.7 124.6 all-gather.7
  762.3 124.6 all-gather.9
  913.8 72.4 all-gather.11
where the time goes:
time: 1020 us
  waiting for transfers between devices  782 us (77%)
  matrix products  148 us (15%)
  blocking collectives  37.3 us (4%)
  local copies, waits for them, and re-layouts  33.2 us (3%)
  between operations  15.4 us (2%)
    all_gather x4, waiting for transfers between devices, local(): whole = lax.all_gather(iterate, 'dp', axis=0, tiled=True)  422 us
    psum x1, waiting for transfers between devices, local(): lax.psum(jnp.einsum('tkr,tkc->rkc', blocks, blocks, preferred_element_typ...  301 us
    all_gather x1, waiting for transfers between devices, local(): lax.all_gather(inverse, 'dp', axis=0, tiled=True)  59.4 us
    dot_general x4, matrix products, local(): jnp.einsum('rkj,jkc->rkc', factor, whole, precision=lax.Precision.HIGHEST)  57 us
    dot_general x4, matrix products, local(): jnp.einsum('rkj,jkc->rkc', product, whole, precision=lax.Precision.HIGHEST)  48 us
    psum x1, blocking collectives, local(): block_squares = lax.psum(jnp.sum(factor * factor, axis=(0, 2)), 'dp')  31.8 us
    dot_general x1, matrix products, local(): jnp.einsum('rkc,kcf->krf', lax.all_gather(inverse, 'dp', axis=0, tiled=Tr...  25.9 us
  transfers between devices with their start and end apart: 6, of which 6 were waited for; matrix products, arithmetic and copies ran while one was open for 1% of the time, Pallas kernels for 0%

commit v1 on v0

--- a/solution.py
+++ b/solution.py
@@ -1,11 +1,35 @@
+import functools
 import jax
 import jax.numpy as jnp
 from jax import lax
 from jax.sharding import PartitionSpec as P
+from jax.lax import axis_index, axis_size, ppermute
 
 BLOCK = 1024
 LAYERS = 2
 ITERS = 4
+
+
+def _process_things(packet, array_axis):
+    parts_n = axis_size("dp")
+    series = [packet]
+    for no in range(parts_n - 1):
+        series.append(
+            ppermute(
+                series[-1],
+                axis_name="dp",
+                perm=[(src_i, (src_i + 1) % parts_n) for src_i in range(parts_n)],
+            )
+        )
+    w_next = jnp.roll(
+        jnp.concatenate(series[::-1], axis=array_axis),
+        (axis_index("dp") + 1) * packet.shape[array_axis],
+        array_axis,
+    )
+    return w_next
+
+
+_plan_axis_part = functools.partial(_process_things, array_axis=0)
 
 
 def local(step, activations, grad_weight):
@@ -33,7 +57,7 @@
     largest = lax.pmax(jnp.max(block_squares), "tensor")
     iterate = jnp.broadcast_to(identity / jnp.sqrt(largest), factor.shape)
     for sweep in range(ITERS):
-        whole = lax.all_gather(iterate, "dp", axis=0, tiled=True)
+        whole = _plan_axis_part(iterate)
         product = jnp.einsum("rkj,jkc->rkc", factor, whole, precision=lax.Precision.HIGHEST)
         iterate = 2.0 * iterate - jnp.einsum(
             "rkj,jkc->rkc", product, whole, precision=lax.Precision.HIGHEST

time: 1020 us -> 1740 us (1.71)
  waiting for transfers between devices: 782 us -> 1370 us
  local copies, waits for them, and re-layouts: 33.2 us -> 123 us
  matrix products: 148 us -> 176 us
    ppermute x0 -> x60, waiting for transfers between devices: none -> 1020 us  [_process_things(): ppermute(series[-1], axis_name='dp', perm=[(src_i, (src_i + 1) % parts_n)...]
    all_gather x4 -> x0, waiting for transfers between devices: 422 us -> none  [local(): whole = lax.all_gather(iterate, 'dp', axis=0, tiled=True)]
    unnamed x13 -> x93, local copies, waits for them, and re-layouts: 12 us -> 97.3 us
    dot_general x4, matrix products: 48 us -> 66.3 us  [local(): jnp.einsum('rkj,jkc->rkc', product, whole, precision=lax.Precision.HIGHEST)]
  transfers between devices with their start and end apart: 6 -> 62, of which waited for: 6 -> 62; matrix products, arithmetic and copies ran while one was open for 1% -> 1% of each run, Pallas kernels for 0% -> 0%
where the time goes in v1:
time: 1740 us; the launch traced here: 1730 us
  waiting for transfers between devices  1370 us (79%)
  matrix products  176 us (10%)
  local copies, waits for them, and re-layouts  123 us (7%)
  blocking collectives  37.3 us (2%)
    ppermute x60, waiting for transfers between devices, _process_things(): ppermute(series[-1], axis_name='dp', perm=[(src_i, (src_i + 1) % parts_n)...  1020 us
    psum x1, waiting for transfers between devices, local(): lax.psum(jnp.einsum('tkr,tkc->rkc', blocks, blocks, preferred_element_typ...  300 us
    unnamed x93, local copies, waits for them, and re-layouts  97.3 us
    dot_general x4, matrix products, local(): jnp.einsum('rkj,jkc->rkc', factor, whole, precision=lax.Precision.HIGHEST)  67 us
    dot_general x4, matrix products, local(): jnp.einsum('rkj,jkc->rkc', product, whole, precision=lax.Precision.HIGHEST)  66.3 us
    all_gather x1, waiting for transfers between devices, local(): lax.all_gather(inverse, 'dp', axis=0, tiled=True)  58.4 us
  transfers between devices with their start and end apart: 62, of which 62 were waited for; matrix products, arithmetic and copies ran while one was open for 1% of the time, Pallas kernels for 0%

profile of v1, /device:TPU:0, one launch (start us, length us, event | category | flops | bytes accessed | tf_op | source)
XLA Modules:
  0.0 1730.1 jit_solution(13687268420460057141)
XLA Ops:
  27.1 17.2 convolution_bitcast_fusion
  44.6 300.5 %all-reduce.2.cloned.1.call-done = f32[1024,4,1024]{0,2,1:T(8,128)} async-done(((f32[1024,4,1024]{0,2,1:T(8,128)}), f32[1024,4,1024]{0,2,1:T(8,128)}) %all-reduce.2.cloned.1.call-update) | async-done | bytes 16777232 | tf_op jit(solution)/shard_map/psum | solution.py:48
  347.4 31.8 %psum.15 = f32[4]{0:T(128)S(1)} all-reduce(f32[4]{0:T(128)S(1)} %multiply_reduce_fusion), channel_id=1, replica_groups=mesh['dp'=16,'tensor'=2] {'dp'}, use_global_device_ids=true, to_apply=%region_2.3 | all-reduce | flops 4 | bytes 32 | tf_op jit(solution)/shard_map/psum | solution.py:56
  403.2 16.9 collective-permute-done.1
  420.1 16.9 collective-permute-done.2
  438.1 16.9 collective-permute-done.3
  456.0 16.9 collective-permute-done.4
  473.9 16.9 collective-permute-done.5
  491.8 16.9 collective-permute-done.6
  509.7 16.9 collective-permute-done.7
  527.7 16.9 collective-permute-done.8
  545.6 16.9 collective-permute-done.9
  563.5 16.9 collective-permute-done.10
  581.4 16.9 collective-permute-done.11
  599.3 16.9 collective-permute-done.12
  617.2 17.0 collective-permute-done.13
  634.3 17.2 collective-permute-done.14
  678.5 17.0 fusion.41
  728.9 16.9 collective-permute-done.16
  745.8 16.9 collective-permute-done.17
  762.7 16.9 collective-permute-done.18
  779.6 16.9 collective-permute-done.19
  796.5 16.9 collective-permute-done.20
  813.5 16.9 collective-permute-done.21
  830.4 16.9 collective-permute-done.22
  847.3 16.9 collective-permute-done.23
  864.2 16.9 collective-permute-done.24
  881.1 16.9 collective-permute-done.25
  898.1 16.9 collective-permute-done.26
  915.0 16.9 collective-permute-done.27
  931.9 16.9 collective-permute-done.28
  948.8 16.9 collective-permute-done.29
  1016.3 16.9 collective-permute-done.30
  1033.2 16.9 collective-permute-done.31
  1050.2 16.9 collective-permute-done.32
  1067.1 16.9 collective-permute-done.33
  1084.0 16.9 collective-permute-done.34
  1100.9 16.9 collective-permute-done.35
  1117.9 16.9 collective-permute-done.36
  1134.8 16.9 collective-permute-done.37
  1151.7 16.9 collective-permute-done.38
  1168.6 16.9 collective-permute-done.39
  1185.5 16.9 collective-permute-done.40
  1202.5 16.9 collective-permute-done.41
  1219.4 16.9 collective-permute-done.42
  1236.3 16.9 collective-permute-done.43
  1253.2 16.9 collective-permute-done.44
  1337.7 16.9 collective-permute-done.46
  1354.6 16.9 collective-permute-done.47
  1371.6 16.9 collective-permute-done.48
  1388.5 16.9 collective-permute-done.49
  1405.4 16.9 collective-permute-done.50
  1422.3 16.9 collective-permute-done.51
  1439.2 16.9 collective-permute-done.52
  1456.2 16.9 collective-permute-done.53
  1473.1 16.9 collective-permute-done.54
  1490.0 16.9 collective-permute-done.55
  1506.9 16.9 collective-permute-done.56
  1523.8 16.9 collective-permute-done.57
  1540.8 16.9 collective-permute-done.58
  1557.7 16.9 collective-permute-done.59
  1608.4 17.3 subtract_convert_fusion
  1639.0 58.4 %all-gather.2.cloned.1.call-done = bf16[1024,4,1024]{2,0,1:T(8,128)(2,1)} async-done(((bf16[64,4,1024]{2,0,1:T(8,128)(2,1)}), bf16[1024,4,1024]{2,0,1:T(8,128)(2,1)}) %all-gather.2.cloned.1.call-update) | async-done | bytes 8388624 | tf_op jit(solution)/shard_map/all_gather | solution.py:69
  1697.4 25.7 %fusion.71 = f32[4,1024,1792]{2,1,0:T(8,128)} fusion(bf16[1024,4,1024]{2,0,1:T(8,128)(2,1)} %all-gather.2.cloned.1.call-done, bf16[4,1024,1792]{2,1,0:T(8,128)(2,1)} %bitcast.42), kind=kOutput, calls=%fused_computation.122 | convolution fusion | flops 15032385536 | bytes 52428800 | tf_op jit(solution)/shard_map/rkc,kcf->krf/dot_general | solution.py:67
  (180 shorter events, 282.4 us)
Async XLA Ops:
  6.5 338.6 %all-reduce.2.cloned.1.call-start = ((), (), s32[]{:S(2)}) async-start(), calls=%async_computation | async-start | bytes 33554432 | tf_op jit(solution)/shard_map/psum | solution.py:48
  44.3 1653.2 %all-gather.2.cloned.1.call-start = ((), (), s32[]{:S(2)}) async-start(), calls=%async_computation.1 | async-start | bytes 8912896 | tf_op jit(solution)/shard_map/all_gather | solution.py:69
  386.3 17.0 collective-permute-start
  403.2 16.9 collective-permute-start.1
  420.1 16.9 collective-permute-start.2
  438.1 16.9 collective-permute-start.3
  456.0 16.9 collective-permute-start.4
  473.9 16.9 collective-permute-start.5
  491.8 16.9 collective-permute-start.6
  509.7 16.9 collective-permute-start.7
  527.7 16.9 collective-permute-start.8
  545.6 16.9 collective-permute-start.9
  563.5 16.9 collective-permute-start.10
  581.4 16.9 collective-permute-start.11
  599.3 16.9 collective-permute-start.12
  617.2 17.0 collective-permute-start.13
  634.2 17.2 collective-permute-start.14
  634.3 38.9 %copy-start.3 = (f32[64,4,1024]{2,0,1:T(8,128)S(1)}, f32[64,4,1024]{2,0,1:T(8,128)}, u32[]{:S(2)}) copy-start(f32[64,4,1024]{2,0,1:T(8,128)} %copy-done.2) | copy-start | bytes 3145732
  634.3 40.0 %copy-start.1 = (f32[64,4,1024]{2,0,1:T(8,128)S(1)}, f32[64,4,1024]{2,0,1:T(8,128)}, u32[]{:S(2)}) copy-start(f32[64,4,1024]{2,0,1:T(8,128)} %copy-done) | copy-start | bytes 3145732
  711.9 17.0 collective-permute-start.15
  728.8 16.9 collective-permute-start.16
  745.8 16.9 collective-permute-start.17
  762.7 16.9 collective-permute-start.18
  779.6 16.9 collective-permute-start.19
  796.5 16.9 collective-permute-start.20
  813.5 16.9 collective-permute-start.21
  830.4 16.9 collective-permute-start.22
  847.3 16.9 collective-permute-start.23
  864.2 16.9 collective-permute-start.24
  881.1 16.9 collective-permute-start.25
  898.1 16.9 collective-permute-start.26
  915.0 16.9 collective-permute-start.27
  931.9 16.9 collective-permute-start.28
  948.8 16.9 collective-permute-start.29
  1016.1 17.2 collective-permute-start.30
  1033.2 16.9 collective-permute-start.31
  1050.2 16.9 collective-permute-start.32
  1067.1 16.9 collective-permute-start.33
  1084.0 16.9 collective-permute-start.34
  1100.9 16.9 collective-permute-start.35
  1117.9 16.9 collective-permute-start.36
  1134.8 16.9 collective-permute-start.37
  1151.7 16.9 collective-permute-start.38
  1168.6 16.9 collective-permute-start.39
  1185.5 16.9 collective-permute-start.40
  1202.5 16.9 collective-permute-start.41
  1219.4 16.9 collective-permute-start.42
  1236.3 16.9 collective-permute-start.43
  1253.2 16.9 collective-permute-start.44
  1320.3 17.4 %collective-permute-start.45 = (f32[64,4,1024]{2,0,1:T(8,128)S(1)}, f32[64,4,1024]{2,0,1:T(8,128)S(1)}, u32[]{:S(2)}, u32[]{:S(2)}) collective-permute-start(f32[64,4,1024]{2,0,1:T(8,128)S(1)} %multiply_subtract_fusion), channel_id=1, source_target_pairs={{0,2},{2,4},{4,6},{6,8},{8,10},{10,12},{12,14},{14,16},{16,18},{18... | collective-permute-start | bytes 3145736 | tf_op jit(solution)/shard_map/ppermute | solution.py:18
  1337.7 16.9 collective-permute-start.46
  1354.6 16.9 collective-permute-start.47
  1371.6 16.9 collective-permute-start.48
  1388.5 16.9 collective-permute-start.49
  1405.4 16.9 collective-permute-start.50
  1422.3 16.9 collective-permute-start.51
  1439.2 16.9 collective-permute-start.52
  1456.2 16.9 collective-permute-start.53
  1473.1 16.9 collective-permute-start.54
  1490.0 16.9 collective-permute-start.55
  1506.9 16.9 collective-permute-start.56
  1523.8 16.9 collective-permute-start.57
  1540.8 16.9 collective-permute-start.58
  1557.7 16.9 collective-permute-start.59
  (14 other events, 121.2 us)
Sparse Core Ops, SparseCore 0:
  44.4 300.6 all-reduce.1
  1625.8 71.5 all-gather.1
